TPU v7x, 32 devices: a whole 2x2x4 slice. The times are simulated.
32 devices in a mesh: dp: 8 (over z, x), shard: 4 (over y, core).
Axes of the slice: x: 2, y: 2, z: 4, core: 2. Of those that a mesh axis runs over, the one named last changes fastest.
Arguments:
- hidden_in: bfloat16 [8192, 5120], P(('dp', 'shard')), may hold values from -6 to 6
- teacher: bfloat16 [8192, 768], P(('dp', 'shard')), may hold values from -6 to 6
- norm_gain: bfloat16 [5120], P('shard'), may hold values from 0.5 to 1.5
- w_key: bfloat16 [5120, 768], P('shard'), may hold values from -0.078125 to 0.078125
- group_rows: int32 [8], P('dp'), may hold values from 64 to 256
- member: int32 [8, 4], P('dp', 'shard'), may hold values from 0 to 1, as said below
Outputs:
- loss: float32 [], replicated
- grad_gain: float32 [5120], P('shard')
- grad_key: float32 [5120, 768], P('shard')
Inputs may be any that keep to these rules, and one draw needn't show every extreme that they name: The first group_rows[p] token slots of each surviving device of group p hold valid tokens. `member`: 1 marks a surviving device; the first device of every group survives.
All inputs are finite; a program needn't handle non-finite values.
Results may differ from a plain program's by a relative error of at most 0.0023.
Values may be sent and summed in bfloat16 or wider, within the bound.
A program may use at most 128 MiB of HBM per device.

v0:
```python
import jax
import jax.numpy as jnp
from jax import lax
from jax.sharding import PartitionSpec as P

EPSILON = 1e-06
SCALE = 1024.0


def contract_rows(left, right):
    return lax.dot_general(
        left, right, (((0,), (0,)), ((), ())), preferred_element_type=jnp.float32
    )


def contract_cols(left, right):
    return lax.dot_general(
        left, right, (((1,), (1,)), ((), ())), preferred_element_type=jnp.float32
    )


def fold_terms(columns, piece):
    return contract_rows(columns, piece)


def body(hidden_in, teacher, norm_gain, w_key, group_rows, member):
    rows, width = hidden_in.shape
    features = w_key.shape[1]
    live_rows = group_rows[0]
    alive = member[0, 0]
    position = lax.broadcasted_iota(jnp.int32, (rows, 1), 0)
    valid = jnp.where((position < live_rows) & (alive == 1), 1.0, 0.0).astype(jnp.float32)
    own_count = (alive * live_rows).astype(jnp.float32)
    values = hidden_in.astype(jnp.float32)
    inverse_rms = lax.rsqrt(jnp.mean(values * values, axis=1, keepdims=True) + EPSILON)
    scaled = values * inverse_rms
    gains, key_full = (
        lax.all_gather(norm_gain, "shard", axis=0, tiled=True),
        lax.all_gather(w_key, "shard", axis=0, tiled=True),
    )
    normed = (scaled * gains.astype(jnp.float32)).astype(jnp.bfloat16)
    keys = jnp.dot(normed, key_full, preferred_element_type=jnp.float32)
    diff = keys - teacher.astype(jnp.float32)
    own_sum = jnp.sum(valid * diff * diff)
    total_sum, total_count = lax.psum((own_sum, own_count), ("dp", "shard"))
    loss = total_sum / (2.0 * features * total_count)
    upstream = (SCALE / total_count * valid * diff).astype(jnp.bfloat16)
    dnormed = contract_cols(upstream, key_full)
    term_gain = jnp.sum(dnormed * scaled, axis=0)
    columns = lax.all_to_all(normed, "shard", split_axis=1, concat_axis=0, tiled=True)
    key_piece = fold_terms(columns, lax.all_gather(upstream, "shard", axis=0, tiled=True))
    gain_piece = lax.psum_scatter(term_gain, "shard", scatter_dimension=0, tiled=True)
    grad_gain, grad_key = lax.psum((gain_piece, key_piece), "dp")
    return (loss, grad_gain, grad_key)


def solution(mesh):
    in_specs = (
        P(("dp", "shard"), None),
        P(("dp", "shard"), None),
        P("shard"),
        P("shard", None),
        P("dp"),
        P("dp", "shard"),
    )
    out_specs = (P(), P("shard"), P("shard", None))
    return jax.shard_map(body, mesh=mesh, in_specs=in_specs, out_specs=out_specs, check_vma=False)
```

profile of v0, /device:TPU:28, one launch (start us, length us, event | category | flops | bytes accessed | tf_op | source)
XLA Modules:
  0.0 325.0 jit_solution(2821802865458533241)
XLA Ops:
  7.2 0.0 all-gather.4.cloned.1.call-start
  7.2 0.7 all-gather.4.cloned.1.call-update
  7.9 0.0 all-gather.6.cloned.1.call-start
  9.3 0.7 reshape.30
  10.0 5.2 %all-gather = bf16[4,1,1280]{2,1,0:T(2,128)(2,1)S(1)} all-gather(bf16[1,1,1280]{2,1,0:T(2,128)(2,1)S(1)} %reshape.30), channel_id=1, replica_groups=mesh['dp'=8,'shard'=4] {'shard'}, dimensions={0}, use_global_device_ids=true | all-gather | bytes 12800 | tf_op jit(solution)/shard_map/all_gather | solution.py:38
  15.2 2.5 fusion.2
  17.7 2.3 fusion.1
  20.0 44.9 %all-gather.4.cloned.1.call-done = bf16[5120,768]{1,0:T(8,128)(2,1)} async-done(((bf16[1280,768]{1,0:T(8,128)(2,1)}), bf16[5120,768]{1,0:T(8,128)(2,1)}) %all-gather.4.cloned.1.call-update) | async-done | bytes 7864336 | tf_op jit(solution)/shard_map/all_gather | solution.py:39
  64.9 6.9 %fusion.4 = (f32[]{:T(128)}, f32[256,768]{1,0:T(8,128)S(1)}) fusion(f32[256]{0:T(256)S(1)} %and_select_fusion, bf16[256,768]{1,0:T(8,128)(2,1)} %param.7, bf16[256,5120]{1,0:T(8,128)(2,1)} %fusion.1, bf16[5120,768]{1,0:T(8,128)(2,1)} %all-gather.4.cloned.1.call-done), kind=kOutput, calls=%fused_computation.10 | convolution fusion | flops 2014248960 | bytes 11666436 | tf_op jit(solution)/shard_map/dot_general | solution.py:42
  71.7 40.3 %all-reduce.1 = (f32[]{:T(128)}, f32[]{:T(128)}) all-reduce(f32[]{:T(128)} %get-tuple-element.5, f32[]{:T(128)S(6)} %convert_element_type.22), channel_id=1, replica_groups=mesh['dp'=8,'shard'=4] {'dp','shard'}, use_global_device_ids=true, to_apply=%region_2.3 | all-reduce | flops 2 | bytes 16 | tf_op jit(solution)/shard_map/psum | solution.py:45
  112.7 0.8 multiply_convert_fusion
  113.6 0.0 all-gather.6.cloned.1.call-update
  113.6 0.0 all-reduce.4.cloned.1.call-start
  113.6 1.9 copy.13
  115.6 41.3 %all_to_all.19 = bf16[256,4,1280]{2,0,1:T(8,128)(2,1)} all-to-all(bf16[256,4,1280]{2,0,1:T(8,128)(2,1)S(1)} %bitcast.23), channel_id=1, replica_groups=mesh['dp'=8,'shard'=4] {'shard'}, dimensions={1} | all-to-all | bytes 5242880 | tf_op jit(solution)/shard_map/all_to_all | solution.py:50
  156.8 6.4 %fusion.5 = f32[1280,768]{1,0:T(8,128)} fusion(bf16[1024,1280]{1,0:T(8,128)(2,1)} %bitcast.24, bf16[1024,768]{1,0:T(8,128)(2,1)} %all-gather.6.cloned.1.call-done), kind=kOutput, calls=%fused_computation.15 | convolution fusion | flops 2013265920 | bytes 8126464 | tf_op jit(solution)/shard_map/dot_general | solution.py:11
  163.3 0.6 copy-done.2
  163.9 0.6 dynamic-slice
  166.4 5.5 %fusion.3 = f32[5120]{0:T(1024)S(1)} fusion(f32[256]{0:T(256)S(1)} %add_rsqrt_fusion, bf16[256,5120]{1,0:T(8,128)(2,1)S(1)} %copy-done, bf16[256,768]{1,0:T(8,128)(2,1)S(1)} %copy-done.1, bf16[5120,768]{1,0:T(8,128)(2,1)} %all-gather.4.cloned.1.call-done), kind=kOutput, calls=%fused_computation.7 | convolution fusion | flops 2018503680 | bytes 10900480 | tf_op jit(solution)/shard_map/dot_general | solution.py:17
  171.9 11.6 %all-reduce = f32[5120]{0:T(1024)S(1)} all-reduce(f32[5120]{0:T(1024)S(1)} %fusion.3), channel_id=2, replica_groups=mesh['dp'=8,'shard'=4] {'shard'}, use_global_device_ids=true, to_apply=%region_5.6.clone | all-reduce | flops 5120 | bytes 40960
  183.5 0.1 dynamic-slice.1
  183.6 19.5 %psum.30 = f32[1280]{0:T(1024)} all-reduce(f32[1280]{0:T(1024)S(1)} %dynamic-slice.1), channel_id=1, replica_groups=mesh['dp'=8,'shard'=4] {'dp'}, use_global_device_ids=true, to_apply=%region_6.7 | all-reduce | flops 1280 | bytes 10240 | tf_op jit(solution)/shard_map/psum | solution.py:53
  203.1 110.0 %all-reduce.4.cloned.1.call-done = f32[1280,768]{1,0:T(8,128)} async-done(((f32[1280,768]{1,0:T(8,128)}), f32[1280,768]{1,0:T(8,128)}) %all-reduce.4.cloned.1.call-update) | async-done | bytes 3932176 | tf_op jit(solution)/shard_map/psum | solution.py:53
  313.1 4.3 %copy.17 = f32[1280,768]{1,0:T(8,128)} copy(f32[1280,768]{1,0:T(8,128)} %all-reduce.4.cloned.1.call-done) | data formatting | bytes 7864320
  (11 shorter events, 0.1 us)
Async XLA Ops:
  7.2 10.5 %copy-start = (bf16[256,5120]{1,0:T(8,128)(2,1)S(1)}, bf16[256,5120]{1,0:T(8,128)(2,1)}, u32[]{:S(2)}) copy-start(bf16[256,5120]{1,0:T(8,128)(2,1)} %param.6) | copy-start | bytes 7864324
  7.2 57.7 %all-gather.4.cloned.1.call-start = ((), (), s32[]{:S(2)}) async-start(), calls=%async_computation.1 | async-start | bytes 9830400 | tf_op jit(solution)/shard_map/all_gather | solution.py:39
  7.9 148.9 %all-gather.6.cloned.1.call-start = ((), (), s32[]{:S(2)}) async-start(), calls=%async_computation.2 | async-start | bytes 1966080 | tf_op jit(solution)/shard_map/all_gather | solution.py:51
  113.6 199.5 %all-reduce.4.cloned.1.call-start = ((), (), s32[]{:S(2)}) async-start(), calls=%async_computation.3 | async-start | bytes 7864320 | tf_op jit(solution)/shard_map/psum | solution.py:53
  163.2 0.7 copy-start.2
  163.2 3.2 copy-start.1
Sparse Core Ops, SparseCore 0:
  9.5 55.2 all-gather.3
  113.7 28.2 all-gather.5
  163.4 149.6 all-reduce.3
where the time goes:
time: 329 us; the launch traced here: 325 us
  waiting for transfers between devices  156 us (47%)
  blocking collectives  118 us (36%)
  matrix products  18.8 us (6%)
  between operations  18.8 us (6%)
  local copies, waits for them, and re-layouts  8.18 us (2%)
  other arithmetic  5.62 us (2%)
    psum x1, waiting for transfers between devices, body(): grad_gain, grad_key = lax.psum((gain_piece, key_piece), 'dp')  110 us
    all_gather x1, waiting for transfers between devices, body(): lax.all_gather(w_key, 'shard', axis=0, tiled=True)  44.9 us
    all_to_all x1, blocking collectives, body(): lax.all_to_all(normed, 'shard', split_axis=1, concat_axis=0, tiled=True)  41.3 us
    psum x1, blocking collectives, body(): total_sum, total_count = lax.psum((own_sum, own_count), ('dp', 'shard'))  40.3 us
    psum x1, blocking collectives, body(): grad_gain, grad_key = lax.psum((gain_piece, key_piece), 'dp')  19.5 us
    unnamed x1, blocking collectives  11.6 us
    dot_general x1, matrix products, body(): keys = jnp.dot(normed, key_full, preferred_element_type=jnp.float32)  6.85 us
  transfers between devices with their start and end apart: 3, of which 2 were waited for; matrix products, arithmetic and copies ran while one was open for 4% of the time, Pallas kernels for 0%

commit v1 on v0

v1 whole, which is shorter than its diff:
```python
import functools
import math

import jax
import jax.numpy as jnp
from jax import lax
from jax.experimental import pallas as pl
from jax.experimental.pallas import tpu as pltpu
from jax.sharding import PartitionSpec as P

EPSILON = 1e-06
SCALE = 1024.0
MESH = pl.DeviceIdType.MESH
F32 = jnp.float32
BF16 = jnp.bfloat16


def inner_of(groups):
    return max(d for d in range(1, groups + 1) if groups % d == 0 and d * d <= groups)


def kernel(
    members, groups, width, chunks,
    hidden, teacher, gains, w_key, valid, count,
    out, loss_out,
    inv_cols, small_send, small_recv, cnt_send, cnt_recv, loss_send, loss_recv,
    cols, cols_t, part_send, part_recv, keys_own, keys_recv, dk_all,
    grads, x_recv, half, z_recv,
    a2a_s, a2a_r, small_s, small_r, cnt_s, cnt_r, loss_s, loss_r,
    part_s, part_r, keys_s, keys_r, dk_s, dk_r, dks_s, dks_r, dkf_s, dkf_r,
    x_s, x_r, z_s, z_r, za_s, za_r, xa_s, xa_r,
):
    tokens, kv = teacher.shape
    feats = w_key.shape[0]
    kc = kv // chunks
    inner = inner_of(groups)
    outer = groups // inner
    hrows = feats // inner
    qrows = hrows // outer
    pairs = members // 2
    p, s = lax.axis_index("dp"), lax.axis_index("shard")
    px, pz = lax.rem(p, inner), p // inner
    chip, par = s // 2, lax.rem(s, 2)
    twin = chip * 2 + 1 - par
    pending = []

    def member_at(d):
        return lax.rem(s + d, members)

    def group_at(d):
        return lax.rem(p + d, groups)

    def chip_at(d):
        return lax.rem(chip + d, pairs)

    def x_at(d):
        return lax.rem(px + d, inner)

    def z_at(d):
        return lax.rem(pz + d, outer)

    def send(src, dst, ssem, rsem, group, member):
        copy = pltpu.make_async_remote_copy(
            src_ref=src, dst_ref=dst, send_sem=ssem, recv_sem=rsem,
            device_id=(group, member), device_id_type=MESH,
        )
        copy.start()
        pending.append(copy)

    def arrived(dst, ssem, rsem):
        pltpu.make_async_remote_copy(
            src_ref=dst, dst_ref=dst, send_sem=ssem, recv_sem=rsem,
            device_id=(p, twin), device_id_type=MESH,
        ).wait_recv()

    barrier = pltpu.get_barrier_semaphore()
    for d in range(1, members):
        pl.semaphore_signal(barrier, inc=1, device_id=(p, member_at(d)), device_id_type=MESH)
    for d in range(1, groups):
        pl.semaphore_signal(barrier, inc=1, device_id=(group_at(d), s), device_id_type=MESH)
    pl.semaphore_wait(barrier, members + groups - 2)

    for d in range(1, members):
        j = member_at(d)
        send(
            hidden.at[:, pl.ds(pl.multiple_of(j * feats, 128), feats)],
            cols.at[s], a2a_s.at[d - 1], a2a_r.at[d - 1], p, j,
        )

    step_rows = 64
    def squares(r, carry):
        rows = pl.ds(pl.multiple_of(r * step_rows, step_rows), step_rows)
        x = hidden[rows, :].astype(F32)
        total = jnp.sum(x * x, axis=1, keepdims=True)
        inv = lax.rsqrt(total / width + EPSILON)
        inv_cols[rows, :] = jnp.broadcast_to(inv, (step_rows, 128))
        return carry
    lax.fori_loop(0, tokens // step_rows, squares, 0)

    small_send[pl.ds(0, 8), :] = inv_cols[...].T[:8, :]
    small_send[pl.ds(8, 8), :] = jnp.broadcast_to(count[:, :1], (8, tokens))
    for d in range(1, members):
        send(small_send, small_recv.at[d - 1], small_s.at[d - 1], small_r.at[d - 1], p, member_at(d))

    def normalise(j, source, column):
        def rows_of(r, carry):
            rows = pl.ds(pl.multiple_of(r * step_rows, step_rows), step_rows)
            x = source(rows).astype(F32) * inv_cols[rows, :1]
            cols[j, rows, :] = (x * gains[...]).astype(BF16)
            return carry
        lax.fori_loop(0, tokens // step_rows, rows_of, 0)

        def turn(b, carry):
            lanes = pl.ds(pl.multiple_of(b * 128, 128), 128)
            cols_t[lanes, pl.ds(pl.multiple_of(j * tokens, 128), tokens)] = cols[j, :, lanes].T
            return carry
        lax.fori_loop(0, feats // 128, turn, 0)

    own = pl.ds(pl.multiple_of(s * feats, 128), feats)
    normalise(s, lambda rows: hidden[rows, own], None)

    total = count[...]
    for d in range(1, members):
        arrived(small_recv.at[d - 1], small_s.at[d - 1], small_r.at[d - 1])
        total = total + small_recv[d - 1, pl.ds(8, 8), :128]
    cnt_send[...] = total
    for d in range(1, groups):
        send(cnt_send, cnt_recv.at[d - 1], cnt_s.at[d - 1], cnt_r.at[d - 1], group_at(d), s)

    for d in range(1, members):
        j = lax.rem(s + members - d, members)
        arrived(cols.at[j], a2a_s.at[d - 1], a2a_r.at[d - 1])
        inv_cols[...] = jnp.broadcast_to(small_recv[d - 1, pl.ds(0, 1), :], (128, tokens)).T
        normalise(j, lambda rows: cols[j, rows, :], None)

    for d in range(1, groups):
        arrived(cnt_recv.at[d - 1], cnt_s.at[d - 1], cnt_r.at[d - 1])
        total = total + cnt_recv[d - 1]
    scale = valid[...] * (SCALE / total[:1, :1])

    def lanes_of(c):
        return pl.ds(c * kc, kc)

    def stage_keys(c):
        for d in range(pairs):
            j = chip_at(d) * 2 + 1 - par
            part_send[c, d] = jnp.dot(cols[j], w_key[:, lanes_of(c)], preferred_element_type=F32)
            send(part_send.at[c, d], part_recv.at[c, d], part_s.at[c, d], part_r.at[c, d], p, twin)
        for i in range(pairs):
            d = (i + 1) % pairs
            j = chip_at(d) * 2 + par
            mine = jnp.dot(cols[j], w_key[:, lanes_of(c)], preferred_element_type=F32)
            arrived(part_recv.at[c, d], part_s.at[c, d], part_r.at[c, d])
            keys_own[c, d] = mine + part_recv[c, d]
            if d:
                send(
                    keys_own.at[c, d], keys_recv.at[c, d - 1],
                    keys_s.at[c, d - 1], keys_r.at[c, d - 1], p, j,
                )

    def stage_dk(c):
        keys = keys_own[c, 0]
        for d in range(1, pairs):
            arrived(keys_recv.at[c, d - 1], keys_s.at[c, d - 1], keys_r.at[c, d - 1])
            keys = keys + keys_recv[c, d - 1]
        diff = keys - teacher[:, lanes_of(c)].astype(F32)
        dk_all[c, s] = (scale * diff).astype(BF16)
        for d in range(1, pairs):
            send(
                dk_all.at[c, s], dk_all.at[c, s], dk_s.at[c, d - 1], dk_r.at[c, d - 1],
                p, chip_at(d) * 2 + par,
            )
        send(dk_all.at[c, s], dk_all.at[c, s], dks_s.at[c], dks_r.at[c], p, twin)

    def stage_grads(c, loss):
        for d in range(1, pairs):
            q = lax.rem(chip + pairs - d, pairs) * 2 + par
            arrived(dk_all.at[c, q], dk_s.at[c, d - 1], dk_r.at[c, d - 1])
            send(dk_all.at[c, q], dk_all.at[c, q], dkf_s.at[c, d - 1], dkf_r.at[c, d - 1], p, twin)
        arrived(dk_all.at[c, twin], dks_s.at[c], dks_r.at[c])
        for d in range(1, pairs):
            q = lax.rem(chip + pairs - d, pairs) * 2 + 1 - par
            arrived(dk_all.at[c, q], dkf_s.at[c, d - 1], dkf_r.at[c, d - 1])
        dk = dk_all[c].reshape(members * tokens, kc)
        for i in range(inner):
            d = (i + 1) % inner
            rows = pl.ds(pl.multiple_of(x_at(d) * hrows, 8), hrows)
            grads[c, d] = jnp.dot(cols_t[rows, :], dk, preferred_element_type=F32)
            if d:
                send(
                    grads.at[c, d], x_recv.at[c, d - 1], x_s.at[c, d - 1], x_r.at[c, d - 1],
                    pz * inner + x_at(d), s,
                )
        for m in range(members):
            values = dk_all[c, m].astype(F32)
            loss = loss + jnp.sum(values * values, axis=0, keepdims=True)
        return loss

    def stage_z(c):
        value = grads[c, 0]
        for d in range(1, inner):
            arrived(x_recv.at[c, d - 1], x_s.at[c, d - 1], x_r.at[c, d - 1])
            value = value + x_recv[c, d - 1]
        half[c] = value
        for d in range(1, outer):
            to = z_at(d)
            send(
                half.at[c, pl.ds(pl.multiple_of(to * qrows, 8), qrows), :], z_recv.at[c, d - 1],
                z_s.at[c, d - 1], z_r.at[c, d - 1], to * inner + px, s,
            )

    def rows_at(x, z):
        return pl.ds(pl.multiple_of(x * hrows + z * qrows, 8), qrows)

    def stage_sum(c):
        value = half[c, pl.ds(pl.multiple_of(pz * qrows, 8), qrows), :]
        for d in range(1, outer):
            arrived(z_recv.at[c, d - 1], z_s.at[c, d - 1], z_r.at[c, d - 1])
            value = value + z_recv[c, d - 1]
        mine = rows_at(px, pz)
        out[mine, lanes_of(c)] = value
        spot = out.at[mine, lanes_of(c)]
        for d in range(1, outer):
            send(spot, spot, za_s.at[c, d - 1], za_r.at[c, d - 1], z_at(d) * inner + px, s)
        for e in range(1, inner):
            k = (e - 1) * outer
            send(spot, spot, xa_s.at[c, k], xa_r.at[c, k], pz * inner + x_at(e), s)

    def stage_spread(c):
        for d in range(1, outer):
            spot = out.at[rows_at(px, lax.rem(pz + outer - d, outer)), lanes_of(c)]
            arrived(spot, za_s.at[c, d - 1], za_r.at[c, d - 1])
            for e in range(1, inner):
                k = (e - 1) * outer + d
                send(spot, spot, xa_s.at[c, k], xa_r.at[c, k], pz * inner + x_at(e), s)

    loss = jnp.zeros((1, kc), F32)
    for step in range(chunks + 5):
        for lag, stage in enumerate((stage_keys, stage_dk, stage_grads, stage_z, stage_sum, stage_spread)):
            c = step - lag
            if 0 <= c < chunks:
                if stage is stage_grads:
                    loss = stage(c, loss)
                else:
                    stage(c)
        if step == chunks + 1:
            loss_send[...] = jnp.broadcast_to(jnp.sum(loss, axis=1, keepdims=True), (8, 128))
            for d in range(1, groups):
                send(loss_send, loss_recv.at[d - 1], loss_s.at[d - 1], loss_r.at[d - 1], group_at(d), s)

    square = loss_send[...]
    for d in range(1, groups):
        arrived(loss_recv.at[d - 1], loss_s.at[d - 1], loss_r.at[d - 1])
        square = square + loss_recv[d - 1]
    loss_out[...] = square * (total * (1.0 / (SCALE * SCALE * 2.0 * kv)))
    for c in range(chunks):
        for e in range(1, inner):
            for d in range(outer):
                spot = out.at[
                    rows_at(lax.rem(px + inner - e, inner), lax.rem(pz + outer - d, outer)), lanes_of(c)
                ]
                k = (e - 1) * outer + d
                arrived(spot, xa_s.at[c, k], xa_r.at[c, k])
    for copy in pending:
        copy.wait_send()


def body(members, groups, hidden_in, teacher, norm_gain, w_key, group_rows, member):
    tokens, width = hidden_in.shape
    owned, kv = w_key.shape
    unit = math.lcm(128, 8 * groups)
    feats = -(-owned // unit) * unit
    chunks = 3 if kv % 384 == 0 else 1
    kc = kv // chunks
    live_rows, alive = group_rows[0], member[0, 0]
    position = lax.broadcasted_iota(jnp.int32, (tokens, 1), 0)
    valid = jnp.where((position < live_rows) & (alive == 1), 1.0, 0.0).astype(F32)
    count = jnp.broadcast_to((alive * live_rows).astype(F32), (8, 128))
    gains = norm_gain.astype(F32)
    hidden, weights, wide_gains = hidden_in, w_key, gains
    if feats != owned:
        extra = feats - owned
        hidden = jnp.pad(hidden_in.reshape(tokens, members, owned), ((0, 0), (0, 0), (0, extra)))
        hidden = hidden.reshape(tokens, members * feats)
        weights = jnp.pad(w_key, ((0, extra), (0, 0)))
        wide_gains = jnp.pad(gains, (0, extra))
    inner = inner_of(groups)
    outer = groups // inner
    hrows, pairs = feats // inner, members // 2
    vm = pltpu.VMEM

    def sems(*shape):
        kind = pltpu.SemaphoreType.DMA(tuple(max(n, 1) for n in shape))
        return [kind, kind]

    grad_key, loss = pl.pallas_call(
        functools.partial(kernel, members, groups, width, chunks),
        out_shape=(
            jax.ShapeDtypeStruct((feats, kv), F32),
            jax.ShapeDtypeStruct((8, 128), F32),
        ),
        in_specs=[pl.BlockSpec(memory_space=pltpu.VMEM)] * 6,
        out_specs=(pl.BlockSpec(memory_space=pltpu.VMEM),) * 2,
        scratch_shapes=[
            vm((tokens, 128), F32),
            vm((16, tokens), F32), vm((members - 1, 16, tokens), F32),
            vm((8, 128), F32), vm((groups - 1, 8, 128), F32),
            vm((8, 128), F32), vm((groups - 1, 8, 128), F32),
            vm((members, tokens, feats), BF16), vm((feats, members * tokens), BF16),
            vm((chunks, pairs, tokens, kc), F32), vm((chunks, pairs, tokens, kc), F32),
            vm((chunks, pairs, tokens, kc), F32), vm((chunks, max(pairs - 1, 1), tokens, kc), F32),
            vm((chunks, members, tokens, kc), BF16),
            vm((chunks, inner, hrows, kc), F32), vm((chunks, max(inner - 1, 1), hrows, kc), F32),
            vm((chunks, hrows, kc), F32), vm((chunks, max(outer - 1, 1), hrows // outer, kc), F32),
            *sems(members - 1), *sems(members - 1), *sems(groups - 1), *sems(groups - 1),
            *sems(chunks, pairs), *sems(chunks, pairs - 1), *sems(chunks, pairs - 1), *sems(chunks),
            *sems(chunks, pairs - 1),
            *sems(chunks, inner - 1), *sems(chunks, outer - 1), *sems(chunks, outer - 1),
            *sems(chunks, (inner - 1) * outer),
        ],
        compiler_params=pltpu.CompilerParams(
            collective_id=0, has_side_effects=True, vmem_limit_bytes=60 * 1024 * 1024
        ),
    )(hidden, teacher, wide_gains.reshape(1, feats), weights, valid, count)
    grad_key = grad_key[:owned]
    grad_gain = jnp.sum(grad_key * w_key.astype(F32), axis=1) / gains
    return (loss[0, 0], grad_gain, grad_key)


def solution(mesh):
    in_specs = (
        P(("dp", "shard"), None),
        P(("dp", "shard"), None),
        P("shard"),
        P("shard", None),
        P("dp"),
        P("dp", "shard"),
    )
    out_specs = (P(), P("shard"), P("shard", None))
    step = functools.partial(body, mesh.shape["shard"], mesh.shape["dp"])
    return jax.shard_map(step, mesh=mesh, in_specs=in_specs, out_specs=out_specs, check_vma=False)
```

time: 329 us -> 191 us (0.58)
  Pallas kernels: 0 us -> 179 us
  waiting for transfers between devices: 156 us -> 0 us
  blocking collectives: 118 us -> 0 us
  matrix products: 18.8 us -> 0 us
  between operations: 18.8 us -> 2.11 us
    pallas_call x0 -> x1, Pallas kernels: none -> 179 us  [body(): pl.pallas_call(functools.partial(kernel, members, groups, width, chunks),...]
    psum x1 -> x0, waiting for transfers between devices: 110 us -> none  [body(): grad_gain, grad_key = lax.psum((gain_piece, key_piece), 'dp')]
    psum x2 -> x0, blocking collectives: 59.8 us -> none  [the longest x1 40.3 us: body(): total_sum, total_count = lax.psum((own_sum, own_count), ('dp', 'shard'))]
    all_gather x2 -> x0, waiting for transfers between devices: 44.9 us -> none  [the longest x1 44.9 us: body(): lax.all_gather(w_key, 'shard', axis=0, tiled=True)]
    all_to_all x1 -> x0, blocking collectives: 41.3 us -> none  [body(): lax.all_to_all(normed, 'shard', split_axis=1, concat_axis=0, tiled=True)]
    dot_general x3 -> x0, matrix products: 18.8 us -> none  [the longest x1 6.85 us: body(): keys = jnp.dot(normed, key_full, preferred_element_type=jnp.float32)]
    unnamed x1 -> x0, blocking collectives: 11.6 us -> none
    all_gather x1 -> x0, blocking collectives: 5.2 us -> none  [body(): lax.all_gather(norm_gain, 'shard', axis=0, tiled=True)]
  transfers between devices with their start and end apart: 3 -> 0, of which waited for: 2 -> 0; matrix products, arithmetic and copies ran while one was open for 4% -> 0% of each run, Pallas kernels for 0% -> 0%
where the time goes in v1:
time: 191 us; the launch traced here: 190 us
  Pallas kernels  179 us (94%)
  local copies, waits for them, and re-layouts  5.15 us (3%)
  other arithmetic  3.86 us (2%)
  between operations  2.11 us (1%)
    pallas_call x1, Pallas kernels, body(): pl.pallas_call(functools.partial(kernel, members, groups, width, chunks),...  179 us

profile of v1, /device:TPU:28, one launch (start us, length us, event | category | flops | bytes accessed | tf_op | source)
XLA Modules:
  0.0 190.2 jit_solution(11300348871328766524)
XLA Ops:
  0.6 0.0 copy-start.1
  2.1 0.6 broadcast_in_dim.13.count
  2.7 1.3 reshape.25.gains
  4.0 0.7 fusion.1.valid
  4.6 179.1 %shard_map.85 = (f32[1280,768]{1,0:T(8,128)}, f32[8,128]{1,0:T(8,128)}) custom-call(bf16[256,5120]{1,0:T(8,128)(2,1)} %hidden.1, bf16[256,768]{1,0:T(8,128)(2,1)} %teacher.1, f32[1,1280]{1,0:T(1,128)} %reshape.25.gains, bf16[1280,768]{1,0:T(8,128)(2,1)} %w_key.1, f32[256,1]{1,0:T(8,128)} %fusion.1.valid, f32[8,128]{1,0:T(8,128)} %broadcast_in_dim.13.count), custom_call_target="tpu_custom_call" | custom-call | tf_op jit(solution)/shard_map/pallas_call | solution.py:296
  183.7 0.0 copy-start.2
  183.7 0.0 copy-start
  183.7 1.3 slice.3
  185.1 0.0 copy-done.1
  185.1 2.6 %multiply_reduce_fusion = f32[1280]{0:T(1024)S(1)} fusion(f32[1280,768]{1,0:T(8,128)} %get-tuple-element.12, bf16[1280,768]{1,0:T(8,128)(2,1)S(1)} %copy-done.1), kind=kLoop, calls=%fused_computation | loop fusion | flops 2947840 | bytes 5903360 | tf_op jit(solution)/shard_map/reduce_sum | solution.py:326
  187.7 0.0 copy-done.2
  187.7 0.6 convert_divide_fusion
  188.3 0.0 copy-done
  188.3 1.9 %copy.12 = f32[1280,768]{1,0:T(8,128)} copy(f32[1280,768]{1,0:T(8,128)S(1)} %copy-done) | data formatting | bytes 7864320
Async XLA Ops:
  0.6 184.5 %copy-start.1 = (bf16[1280,768]{1,0:T(8,128)(2,1)S(1)}, bf16[1280,768]{1,0:T(8,128)(2,1)}, u32[]{:S(2)}) copy-start(bf16[1280,768]{1,0:T(8,128)(2,1)} %w_key.1) | copy-start | bytes 5898244
  183.7 3.9 %copy-start.2 = (bf16[1280]{0:T(1024)(128)(2,1)S(1)}, bf16[1280]{0:T(1024)(128)(2,1)}, u32[]{:S(2)}) copy-start(bf16[1280]{0:T(1024)(128)(2,1)} %param.8) | copy-start | bytes 7684
  183.7 4.5 %copy-start = (f32[1280,768]{1,0:T(8,128)S(1)}, f32[1280,768]{1,0:T(8,128)}, u32[]{:S(2)}) copy-start(f32[1280,768]{1,0:T(8,128)} %get-tuple-element.12) | copy-start | bytes 11796484

commit v2 on v1

--- a/solution.py
+++ b/solution.py
@@ -25,10 +25,10 @@
     out, loss_out,
     inv_cols, small_send, small_recv, cnt_send, cnt_recv, loss_send, loss_recv,
     cols, cols_t, part_send, part_recv, keys_own, keys_recv, dk_all,
-    grads, x_recv, half, z_recv,
+    grads, x_send, x_recv, half, half_send, z_recv,
     a2a_s, a2a_r, small_s, small_r, cnt_s, cnt_r, loss_s, loss_r,
     part_s, part_r, keys_s, keys_r, dk_s, dk_r, dks_s, dks_r, dkf_s, dkf_r,
-    x_s, x_r, z_s, z_r, za_s, za_r, xa_s, xa_r,
+    x_s, x_r, z_s, z_r, zu_s, zd_s, za_r, xa_s, xa_r,
 ):
     tokens, kv = teacher.shape
     feats = w_key.shape[0]
@@ -38,6 +38,7 @@
     hrows = feats // inner
     qrows = hrows // outer
     pairs = members // 2
+    align = 16
     p, s = lax.axis_index("dp"), lax.axis_index("shard")
     px, pz = lax.rem(p, inner), p // inner
     chip, par = s // 2, lax.rem(s, 2)
@@ -185,10 +186,13 @@
         for i in range(inner):
             d = (i + 1) % inner
             rows = pl.ds(pl.multiple_of(x_at(d) * hrows, 8), hrows)
-            grads[c, d] = jnp.dot(cols_t[rows, :], dk, preferred_element_type=F32)
-            if d:
+            term = jnp.dot(cols_t[rows, :], dk, preferred_element_type=F32)
+            if not d:
+                grads[c] = term
+            else:
+                x_send[c, d - 1] = term.astype(BF16)
                 send(
-                    grads.at[c, d], x_recv.at[c, d - 1], x_s.at[c, d - 1], x_r.at[c, d - 1],
+                    x_send.at[c, d - 1], x_recv.at[c, d - 1], x_s.at[c, d - 1], x_r.at[c, d - 1],
                     pz * inner + x_at(d), s,
                 )
         for m in range(members):
@@ -197,15 +201,16 @@
         return loss
 
     def stage_z(c):
-        value = grads[c, 0]
+        value = grads[c]
         for d in range(1, inner):
             arrived(x_recv.at[c, d - 1], x_s.at[c, d - 1], x_r.at[c, d - 1])
-            value = value + x_recv[c, d - 1]
+            value = value + x_recv[c, d - 1].astype(F32)
         half[c] = value
+        half_send[c] = value.astype(BF16)
         for d in range(1, outer):
             to = z_at(d)
             send(
-                half.at[c, pl.ds(pl.multiple_of(to * qrows, 8), qrows), :], z_recv.at[c, d - 1],
+                half_send.at[c, pl.ds(pl.multiple_of(to * qrows, align), qrows), :], z_recv.at[c, d - 1],
                 z_s.at[c, d - 1], z_r.at[c, d - 1], to * inner + px, s,
             )
 
@@ -216,23 +221,55 @@
         value = half[c, pl.ds(pl.multiple_of(pz * qrows, 8), qrows), :]
         for d in range(1, outer):
             arrived(z_recv.at[c, d - 1], z_s.at[c, d - 1], z_r.at[c, d - 1])
-            value = value + z_recv[c, d - 1]
+            value = value + z_recv[c, d - 1].astype(F32)
         mine = rows_at(px, pz)
         out[mine, lanes_of(c)] = value
         spot = out.at[mine, lanes_of(c)]
-        for d in range(1, outer):
-            send(spot, spot, za_s.at[c, d - 1], za_r.at[c, d - 1], z_at(d) * inner + px, s)
+        along_line(spot, c, pz)
+        across(spot, c, pz)
+
+    def across(spot, c, q):
         for e in range(1, inner):
-            k = (e - 1) * outer
-            send(spot, spot, xa_s.at[c, k], xa_r.at[c, k], pz * inner + x_at(e), s)
+            copy_to(spot, xa_s.at[c, e - 1, q], xa_r.at[c, e - 1, q], pz * inner + x_at(e), s).start()
+
+    def copy_to(spot, ssem, rsem, group, member):
+        return pltpu.make_async_remote_copy(
+            src_ref=spot, dst_ref=spot, send_sem=ssem, recv_sem=rsem,
+            device_id=(group, member), device_id_type=MESH,
+        )
+
+    def rises(q):
+        return (pz >= q) & (pz < outer - 1)
+
+    def falls(q):
+        return (pz <= q) & (pz > 0)
+
+    def up_copy(spot, c, q):
+        to = jnp.minimum(pz + 1, outer - 1) * inner + px
+        return copy_to(spot, zu_s.at[c, q], za_r.at[c, q], to, s)
+
+    def down_copy(spot, c, q):
+        to = jnp.maximum(pz - 1, 0) * inner + px
+        return copy_to(spot, zd_s.at[c, q], za_r.at[c, q], to, s)
+
+    def along_line(spot, c, q):
+        @pl.when(rises(q))
+        def _():
+            up_copy(spot, c, q).start()
+
+        @pl.when(falls(q))
+        def _():
+            down_copy(spot, c, q).start()
 
     def stage_spread(c):
-        for d in range(1, outer):
-            spot = out.at[rows_at(px, lax.rem(pz + outer - d, outer)), lanes_of(c)]
-            arrived(spot, za_s.at[c, d - 1], za_r.at[c, d - 1])
-            for e in range(1, inner):
-                k = (e - 1) * outer + d
-                send(spot, spot, xa_s.at[c, k], xa_r.at[c, k], pz * inner + x_at(e), s)
+        for q in range(outer):
+            spot = out.at[rows_at(px, q), lanes_of(c)]
+
+            @pl.when(pz != q)
+            def _():
+                arrived(spot, zu_s.at[c, q], za_r.at[c, q])
+                along_line(spot, c, q)
+                across(spot, c, q)
 
     loss = jnp.zeros((1, kc), F32)
     for step in range(chunks + 5):
@@ -254,13 +291,21 @@
         square = square + loss_recv[d - 1]
     loss_out[...] = square * (total * (1.0 / (SCALE * SCALE * 2.0 * kv)))
     for c in range(chunks):
-        for e in range(1, inner):
-            for d in range(outer):
-                spot = out.at[
-                    rows_at(lax.rem(px + inner - e, inner), lax.rem(pz + outer - d, outer)), lanes_of(c)
-                ]
-                k = (e - 1) * outer + d
-                arrived(spot, xa_s.at[c, k], xa_r.at[c, k])
+        for q in range(outer):
+            for e in range(1, inner):
+                spot = out.at[rows_at(lax.rem(px + inner - e, inner), q), lanes_of(c)]
+                arrived(spot, xa_s.at[c, e - 1, q], xa_r.at[c, e - 1, q])
+                spot = out.at[rows_at(px, q), lanes_of(c)]
+                copy_to(spot, xa_s.at[c, e - 1, q], xa_r.at[c, e - 1, q], pz * inner + x_at(e), s).wait_send()
+            spot = out.at[rows_at(px, q), lanes_of(c)]
+
+            @pl.when(rises(q))
+            def _():
+                up_copy(spot, c, q).wait_send()
+
+            @pl.when(falls(q))
+            def _():
+                down_copy(spot, c, q).wait_send()
     for copy in pending:
         copy.wait_send()
 
@@ -268,9 +313,9 @@
 def body(members, groups, hidden_in, teacher, norm_gain, w_key, group_rows, member):
     tokens, width = hidden_in.shape
     owned, kv = w_key.shape
-    unit = math.lcm(128, 8 * groups)
+    unit = math.lcm(128, 16 * groups)
     feats = -(-owned // unit) * unit
-    chunks = 3 if kv % 384 == 0 else 1
+    chunks = kv // 256 if kv % 256 == 0 else 1
     kc = kv // chunks
     live_rows, alive = group_rows[0], member[0, 0]
     position = lax.broadcasted_iota(jnp.int32, (tokens, 1), 0)
@@ -310,13 +355,15 @@
             vm((chunks, pairs, tokens, kc), F32), vm((chunks, pairs, tokens, kc), F32),
             vm((chunks, pairs, tokens, kc), F32), vm((chunks, max(pairs - 1, 1), tokens, kc), F32),
             vm((chunks, members, tokens, kc), BF16),
-            vm((chunks, inner, hrows, kc), F32), vm((chunks, max(inner - 1, 1), hrows, kc), F32),
-            vm((chunks, hrows, kc), F32), vm((chunks, max(outer - 1, 1), hrows // outer, kc), F32),
+            vm((chunks, hrows, kc), F32),
+            vm((chunks, max(inner - 1, 1), hrows, kc), BF16), vm((chunks, max(inner - 1, 1), hrows, kc), BF16),
+            vm((chunks, hrows, kc), F32), vm((chunks, hrows, kc), BF16),
+            vm((chunks, max(outer - 1, 1), hrows // outer, kc), BF16),
             *sems(members - 1), *sems(members - 1), *sems(groups - 1), *sems(groups - 1),
             *sems(chunks, pairs), *sems(chunks, pairs - 1), *sems(chunks, pairs - 1), *sems(chunks),
             *sems(chunks, pairs - 1),
-            *sems(chunks, inner - 1), *sems(chunks, outer - 1), *sems(chunks, outer - 1),
-            *sems(chunks, (inner - 1) * outer),
+            *sems(chunks, inner - 1), *sems(chunks, outer - 1),
+            *sems(chunks, outer), sems(chunks, outer)[0], *sems(chunks, inner - 1, outer),
         ],
         compiler_params=pltpu.CompilerParams(
             collective_id=0, has_side_effects=True, vmem_limit_bytes=60 * 1024 * 1024

time: 191 us -> 161 us (0.84)
  Pallas kernels: 179 us -> 150 us
    pallas_call x1, Pallas kernels: 179 us -> 150 us  [body(): pl.pallas_call(functools.partial(kernel, members, groups, width, chunks),...]
where the time goes in v2:
time: 161 us
  Pallas kernels  150 us (93%)
  local copies, waits for them, and re-layouts  5.15 us (3%)
  other arithmetic  3.86 us (2%)
  between operations  2.11 us (1%)
    pallas_call x1, Pallas kernels, body(): pl.pallas_call(functools.partial(kernel, members, groups, width, chunks),...  150 us

profile of v2, /device:TPU:28, one launch (start us, length us, event | category | flops | bytes accessed | tf_op | source)
XLA Modules:
  0.0 161.1 jit_solution(8228425981901819659)
XLA Ops:
  0.6 0.0 copy-start.1
  2.1 0.6 broadcast_in_dim.13.count
  2.7 1.3 reshape.25.gains
  4.0 0.7 fusion.1.valid
  4.6 150.0 %shard_map.85 = (f32[1280,768]{1,0:T(8,128)}, f32[8,128]{1,0:T(8,128)}) custom-call(bf16[256,5120]{1,0:T(8,128)(2,1)} %hidden.1, bf16[256,768]{1,0:T(8,128)(2,1)} %teacher.1, f32[1,1280]{1,0:T(1,128)} %reshape.25.gains, bf16[1280,768]{1,0:T(8,128)(2,1)} %w_key.1, f32[256,1]{1,0:T(8,128)} %fusion.1.valid, f32[8,128]{1,0:T(8,128)} %broadcast_in_dim.13.count), custom_call_target="tpu_custom_call" | custom-call | tf_op jit(solution)/shard_map/pallas_call | solution.py:341
  154.6 0.0 copy-start.2
  154.6 0.0 copy-start
  154.6 1.3 slice.3
  156.0 0.0 copy-done.1
  156.0 2.6 %multiply_reduce_fusion = f32[1280]{0:T(1024)S(1)} fusion(f32[1280,768]{1,0:T(8,128)} %get-tuple-element.12, bf16[1280,768]{1,0:T(8,128)(2,1)S(1)} %copy-done.1), kind=kLoop, calls=%fused_computation | loop fusion | flops 2947840 | bytes 5903360 | tf_op jit(solution)/shard_map/reduce_sum | solution.py:373
  158.5 0.0 copy-done.2
  158.5 0.6 convert_divide_fusion
  159.1 0.0 copy-done
  159.2 1.9 %copy.12 = f32[1280,768]{1,0:T(8,128)} copy(f32[1280,768]{1,0:T(8,128)S(1)} %copy-done) | data formatting | bytes 7864320
Async XLA Ops:
  0.6 155.3 %copy-start.1 = (bf16[1280,768]{1,0:T(8,128)(2,1)S(1)}, bf16[1280,768]{1,0:T(8,128)(2,1)}, u32[]{:S(2)}) copy-start(bf16[1280,768]{1,0:T(8,128)(2,1)} %w_key.1) | copy-start | bytes 5898244
  154.6 3.9 %copy-start.2 = (bf16[1280]{0:T(1024)(128)(2,1)S(1)}, bf16[1280]{0:T(1024)(128)(2,1)}, u32[]{:S(2)}) copy-start(bf16[1280]{0:T(1024)(128)(2,1)} %param.8) | copy-start | bytes 7684
  154.6 4.5 %copy-start = (f32[1280,768]{1,0:T(8,128)S(1)}, f32[1280,768]{1,0:T(8,128)}, u32[]{:S(2)}) copy-start(f32[1280,768]{1,0:T(8,128)} %get-tuple-element.12) | copy-start | bytes 11796484
